TPU v7x, 32 devices: a whole 2x2x4 slice. The times are simulated.
32 devices in a mesh: node: 4 (over z), chip: 8 (over y, x, core).
Axes of the slice: x: 2, y: 2, z: 4, core: 2. Of those that a mesh axis runs over, the one named last changes fastest.
Arguments:
- pooled_grad: bfloat16 [2048, 4, 256], P(('node', 'chip')), may hold values from -6 to 6
- grad_scale: bfloat16 [2048, 4], P(('node', 'chip')), may hold values from 0.049804688 to 1
- hot_slot: int32 [2048, 4, 2], P(('node', 'chip')), may hold values from 0 to 511
- send_index: int32 [32, 32, 128], P(('node', 'chip')), may hold values from 0 to 255, as said below
- recv_row: int32 [32, 32, 128], P(('node', 'chip')), may hold values from 0 to 4096, as said below
- cold_weight: float32 [4, 32768, 256], P(None, ('node', 'chip')), may hold values from -3 to 3
- cold_accum: float32 [4, 32768], P(None, ('node', 'chip')), may hold values from 0.5 to 8
- hot_weight: float32 [4, 512, 256], replicated, may hold values from -3 to 3
- hot_accum: float32 [4, 512], replicated, may hold values from 1 to 64
Outputs:
- cold_weight_new: float32 [4, 32768, 256], P(None, ('node', 'chip'))
- cold_accum_new: float32 [4, 32768], P(None, ('node', 'chip'))
- hot_weight_new: float32 [4, 512, 256], replicated
- hot_accum_new: float32 [4, 512], replicated
Inputs may be any that keep to these rules, and one draw needn't show every extreme that they name: send_index and recv_row describe the same lookups: slot c from p to q is filled exactly when recv_row[q, p, c] < 4096, the filled slots of a pair come first, and the table in both entries agrees; some owners receive all 128 slots filled from every sender in every draw. `recv_row`: see send_index; empty slots hold 4096.
All inputs are finite; a program needn't handle non-finite values.
Results may differ from a plain program's by a relative error of at most 0.0003.
Values may be sent and summed in bfloat16 or wider, within the bound.
No kernel may reach another device: no remote copies, remote signals or barrier semaphores. Data moves between devices by JAX's collectives and lax.ppermute only.
A program may use at most 64 MiB of HBM per device.

v0:
```python
import math
import jax
import jax.numpy as jnp
from jax import lax
from jax.sharding import PartitionSpec as P

LEARN_RATE = 0.5


def adagrad(weight, accum, grad):
    accum_new = accum + jnp.mean(grad * grad, axis=-1)
    return (weight - LEARN_RATE * grad / jnp.sqrt(accum_new)[..., None], accum_new)


def per_device(
    pooled_grad,
    grad_scale,
    hot_slot,
    send_index,
    recv_row,
    cold_weight,
    cold_accum,
    hot_weight,
    hot_accum,
):
    b_dev, tables, width = pooled_grad.shape
    devices = send_index.shape[1]
    capacity = send_index.shape[2]
    source_rows = b_dev * tables
    pooled_rows = pooled_grad.reshape(source_rows, width)
    scale_rows = grad_scale.reshape(source_rows, 1)
    chosen = send_index.reshape(devices * capacity)
    selector = (chosen[:, None] == jnp.arange(source_rows, dtype=jnp.int32)[None, :]).astype(
        jnp.bfloat16
    )
    outgoing = jnp.dot(selector, pooled_rows, preferred_element_type=jnp.float32).astype(
        jnp.bfloat16
    )
    out_scale = (
        jnp.dot(selector, scale_rows, preferred_element_type=jnp.float32)
        .astype(jnp.bfloat16)
        .reshape(devices * capacity)
    )
    arrived, arrived_scale = (
        lax.all_to_all(
            outgoing.reshape(devices, capacity, width),
            ("node", "chip"),
            split_axis=0,
            concat_axis=0,
            tiled=True,
        ),
        lax.all_to_all(
            out_scale.reshape(devices, capacity),
            ("node", "chip"),
            split_axis=0,
            concat_axis=0,
            tiled=True,
        ),
    )
    slots = devices * capacity
    arrived_rows = arrived.reshape(slots, width)
    arrived_scale = arrived_scale.reshape(slots)
    targets = recv_row.reshape(slots)
    rows_dev = cold_weight.shape[1]
    local_rows = tables * rows_dev
    block = math.gcd(local_rows, 2048)
    blocks = local_rows // block

    def block_grad(first_row):
        levels = first_row + jnp.arange(block, dtype=jnp.int32)
        weights = jnp.where(
            levels[:, None] == targets[None, :], arrived_scale[None, :], jnp.zeros((), jnp.bfloat16)
        )
        return jnp.dot(weights, arrived_rows, preferred_element_type=jnp.float32)

    starts = jnp.arange(blocks, dtype=jnp.int32) * block
    cold_grad = lax.map(block_grad, starts).reshape(local_rows, width)
    new_weight, new_accum = adagrad(
        cold_weight.reshape(local_rows, width), cold_accum.reshape(local_rows), cold_grad
    )
    cold_weight_new = new_weight.reshape(tables, rows_dev, width)
    cold_accum_new = new_accum.reshape(tables, rows_dev)
    hot_rows = hot_weight.shape[1]
    levels = jnp.arange(hot_rows, dtype=jnp.int32)
    matches = jnp.sum((hot_slot[:, :, :, None] == levels).astype(jnp.float32), axis=2)
    coeffs = (matches * grad_scale.astype(jnp.float32)[:, :, None]).astype(jnp.bfloat16)
    hot_term = jnp.einsum("sth,std->thd", coeffs, pooled_grad, preferred_element_type=jnp.float32)
    hot_grad = lax.psum(hot_term, ("node", "chip"))
    hot_weight_new, hot_accum_new = adagrad(hot_weight, hot_accum, hot_grad)
    return (cold_weight_new, cold_accum_new, hot_weight_new, hot_accum_new)


def solution(mesh):
    placed = (
        P(("node", "chip"), None, None),
        P(("node", "chip"), None),
        P(("node", "chip"), None, None),
        P(("node", "chip"), None, None),
        P(("node", "chip"), None, None),
        P(None, ("node", "chip"), None),
        P(None, ("node", "chip")),
        P(),
        P(),
    )
    return jax.shard_map(
        per_device,
        mesh=mesh,
        in_specs=placed,
        out_specs=(P(None, ("node", "chip"), None), P(None, ("node", "chip")), P(), P()),
        check_vma=False,
    )
```

profile of v0, /device:TPU:0, one launch (start us, length us, event | category | flops | bytes accessed | tf_op | source)
XLA Modules:
  0.0 226.0 jit_solution(1676624236561834407)
XLA Ops:
  7.2 0.8 copy.25
  8.0 0.1 reshape.71
  8.1 1.7 fusion.8
  9.8 0.6 copy.26
  10.4 7.3 %all-to-all-start = ((bf16[32,1,128]{2,1,0:T(2,128)(2,1)}), bf16[32,1,128]{2,1,0:T(2,128)(2,1)S(1)}, u32[]{:S(2)}, u32[]{:S(2)}) async-start(bf16[32,1,128]{2,1,0:T(2,128)(2,1)} %copy.26), calls=%async_computation | async-start | bytes 32768 | tf_op jit(solution)/shard_map/all_to_all | solution.py:52
  17.7 0.9 reshape.68
  18.7 0.0 copy-start.5
  18.7 0.0 copy-start.4
  18.7 0.0 copy-start.1
  18.7 2.8 %convolution_convert_fusion = bf16[4096,256]{1,0:T(8,128)(2,1)} fusion(bf16[256,256]{1,0:T(8,128)(2,1)S(1)} %reshape.68, s32[4096]{0:T(1024)} %bitcast.35), kind=kOutput, calls=%fused_computation.10 | convolution fusion | flops 538968064 | bytes 2244608 | tf_op jit(solution)/shard_map/dot_general | solution.py:36
  21.5 3.4 %all-to-all-done = bf16[32,1,128]{2,1,0:T(2,128)(2,1)S(1)} async-done(((bf16[32,1,128]{2,1,0:T(2,128)(2,1)}), bf16[32,1,128]{2,1,0:T(2,128)(2,1)S(1)}, u32[]{:S(2)}, u32[]{:S(2)}) %all-to-all-start) | async-done | bytes 8224 | tf_op jit(solution)/shard_map/all_to_all | solution.py:52
  24.8 3.5 %all-to-all-start.1 = ((bf16[32,128,256]{2,1,0:T(8,128)(2,1)}), bf16[32,128,256]{2,1,0:T(8,128)(2,1)}, u32[]{:S(2)}, u32[]{:S(2)}) async-start(bf16[32,128,256]{2,1,0:T(8,128)(2,1)} %bitcast.7), calls=%async_computation.1 | async-start | bytes 4194304 | tf_op jit(solution)/shard_map/all_to_all | solution.py:45
  28.3 0.0 copy-start.3
  28.3 0.0 copy-start
  28.3 0.0 all-reduce.2.cloned.1.call-start
  28.4 0.0 copy-done.5
  28.4 0.0 copy-done.4
  28.4 0.2 convert_reduce_fusion
  28.6 0.0 copy-done.1
  28.6 1.9 fusion.11
  30.5 0.0 all-reduce.2.cloned.1.call-update
  30.6 0.0 copy-start.6
  30.6 153.3 %all-reduce.2.cloned.1.call-done = f32[4,512,256]{2,1,0:T(8,128)} async-done(((f32[4,512,256]{2,1,0:T(8,128)}), f32[4,512,256]{2,1,0:T(8,128)}) %all-reduce.2.cloned.1.call-update) | async-done | bytes 2097168 | tf_op jit(solution)/shard_map/psum | solution.py:88
  183.9 1.9 multiply_reduce_fusion.1
  185.8 0.0 copy-done.3
  185.9 0.6 fusion.14
  186.5 0.0 copy-done
  186.5 3.3 %divide_subtract_fusion.1 = f32[4,512,256]{2,1,0:T(8,128)} fusion(f32[4,512,256]{2,1,0:T(8,128)S(1)} %copy-done, f32[4,512,256]{2,1,0:T(8,128)} %all-reduce.2.cloned.1.call-done, f32[4,512]{1,0:T(4,128)S(1)} %get-tuple-element.49), kind=kLoop, calls=%fused_computation.15 | loop fusion | flops 1572864 | bytes 6299648 | tf_op jit(solution)/shard_map/sub | solution.py:12
  189.7 0.0 all-to-all-done.1
  189.7 0.0 copy-done.6
  189.7 18.9 %while.10 = (s32[]{:T(128)}, f32[2,2048,256]{2,1,0:T(8,128)}, s32[2]{0:T(128)S(1)}, s32[1,32,128]{2,1,0:T(8,128)S(1)}, bf16[32,128]{1,0:T(8,128)(2,1)S(1)}, /*index=5*/bf16[4096,256]{1,0:T(8,128)(2,1)}, s32[]{:T(128)}) while((s32[]{:T(128)}, f32[2,2048,256]{2,1,0:T(8,128)}, s32[2]{0:T(128)S(1)}, s32[1,32,128]{2,1,0:T(8,128)S(1)}, ...), condition=%wide.region_1.2_spmd, body=%wide.region_0.1_spmd.sunk | while | flops 4311746560 | bytes 4235869 | solution.py:77
  189.7 0.6 dynamic_slice.5
  190.4 0.7 iota_add_fusion.2
  191.1 8.1 %fusion.22 = f32[2,2048,256]{2,1,0:T(8,128)} fusion(f32[2,2048,256]{2,1,0:T(8,128)} %get-tuple-element.100, s32[]{:T(128)} %get-tuple-element.99, bf16[4096,256]{1,0:T(8,128)(2,1)} %get-tuple-element.111, s32[4096]{0:T(1024)S(1)} %bitcast.36, s32[2048]{0:T(1024)S(1)} %iota_add_fusion.2, bf16[4096]{0:T(1024)(128)(2,1)S(1)} %bitcast.33), kind=kOutput, calls=%fused_computation.7.clone.1 | convolution fusion | flops 4311744512 | bytes 4227584 | tf_op jit(solution)/shard_map/while/body/eval_jaxpr/dot_general | solution.py:74
  199.2 0.6 dynamic_slice.5
  199.8 0.7 iota_add_fusion.2
  200.5 8.1 %fusion.22 = f32[2,2048,256]{2,1,0:T(8,128)} fusion(f32[2,2048,256]{2,1,0:T(8,128)} %get-tuple-element.100, s32[]{:T(128)} %get-tuple-element.99, bf16[4096,256]{1,0:T(8,128)(2,1)} %get-tuple-element.111, s32[4096]{0:T(1024)S(1)} %bitcast.36, s32[2048]{0:T(1024)S(1)} %iota_add_fusion.2, bf16[4096]{0:T(1024)(128)(2,1)S(1)} %bitcast.33), kind=kOutput, calls=%fused_computation.7.clone.1 | convolution fusion | flops 4311744512 | bytes 4227584 | tf_op jit(solution)/shard_map/while/body/eval_jaxpr/dot_general | solution.py:74
  208.6 0.0 copy-start.2
  208.6 4.7 %multiply_reduce_fusion = (f32[2,2048]{1,0:T(2,128)S(1)}, f32[2,2048,256]{2,1,0:T(8,128)}) fusion(f32[2,2048,256]{2,1,0:T(8,128)} %get-tuple-element.36), kind=kLoop, calls=%fused_computation.12 | loop fusion | flops 3141632 | bytes 8404992 | tf_op jit(solution)/shard_map/reduce_sum | solution.py:11
  213.4 0.0 copy-done.2
  213.4 0.6 fusion.15
  214.0 5.1 %divide_subtract_fusion = f32[4,1024,256]{2,1,0:T(8,128)} fusion(f32[4,1024,256]{2,1,0:T(8,128)} %param.16, f32[4,1024,256]{2,1,0:T(8,128)} %bitcast.30, f32[4,1024]{1,0:T(4,128)S(1)} %get-tuple-element.51), kind=kLoop, calls=%fused_computation.11 | loop fusion | flops 2097152 | bytes 12599296 | tf_op jit(solution)/shard_map/sub | solution.py:12
  (7 shorter events, 0.1 us)
Async XLA Ops:
  10.4 14.4 %all-to-all-start = ((bf16[32,1,128]{2,1,0:T(2,128)(2,1)}), bf16[32,1,128]{2,1,0:T(2,128)(2,1)S(1)}, u32[]{:S(2)}, u32[]{:S(2)}) async-start(bf16[32,1,128]{2,1,0:T(2,128)(2,1)} %copy.26), calls=%async_computation | async-start | bytes 32768 | tf_op jit(solution)/shard_map/all_to_all | solution.py:52
  18.7 9.7 %copy-start.5 = (bf16[64,4]{0,1:T(4,128)(2,1)S(1)}, bf16[64,4]{0,1:T(4,128)(2,1)}, u32[]{:S(2)}) copy-start(bf16[64,4]{0,1:T(4,128)(2,1)} %param.12) | copy-start | bytes 1540
  18.7 9.7 %copy-start.4 = (s32[64,4,2]{0,2,1:T(2,128)S(1)}, s32[64,4,2]{0,2,1:T(2,128)}, u32[]{:S(2)}) copy-start(s32[64,4,2]{0,2,1:T(2,128)} %param.13) | copy-start | bytes 6148
  18.7 9.9 %copy-start.1 = (bf16[64,4,256]{2,1,0:T(4,128)(2,1)S(1)}, bf16[64,4,256]{2,1,0:T(4,128)(2,1)}, u32[]{:S(2)}) copy-start(bf16[64,4,256]{2,1,0:T(4,128)(2,1)} %param.11) | copy-start | bytes 393220
  24.8 164.9 %all-to-all-start.1 = ((bf16[32,128,256]{2,1,0:T(8,128)(2,1)}), bf16[32,128,256]{2,1,0:T(8,128)(2,1)}, u32[]{:S(2)}, u32[]{:S(2)}) async-start(bf16[32,128,256]{2,1,0:T(8,128)(2,1)} %bitcast.7), calls=%async_computation.1 | async-start | bytes 4194304 | tf_op jit(solution)/shard_map/all_to_all | solution.py:45
  28.3 157.5 %copy-start.3 = (f32[4,512]{1,0:T(4,128)S(1)}, f32[4,512]{1,0:T(4,128)}, u32[]{:S(2)}) copy-start(f32[4,512]{1,0:T(4,128)} %param.19) | copy-start | bytes 24580
  28.3 158.1 %copy-start = (f32[4,512,256]{2,1,0:T(8,128)S(1)}, f32[4,512,256]{2,1,0:T(8,128)}, u32[]{:S(2)}) copy-start(f32[4,512,256]{2,1,0:T(8,128)} %param.18) | copy-start | bytes 6291460
  28.3 155.6 %all-reduce.2.cloned.1.call-start = ((), (), s32[]{:S(2)}) async-start(), calls=%async_computation.2 | async-start | bytes 4194304 | tf_op jit(solution)/shard_map/psum | solution.py:88
  30.6 159.1 %copy-start.6 = (s32[1,32,128]{2,1,0:T(8,128)S(1)}, s32[1,32,128]{2,1,0:T(8,128)}, u32[]{:S(2)}) copy-start(s32[1,32,128]{2,1,0:T(8,128)} %param.15) | copy-start | bytes 49156
  208.6 4.8 %copy-start.2 = (f32[4,1024]{1,0:T(4,128)S(1)}, f32[4,1024]{1,0:T(4,128)}, u32[]{:S(2)}) copy-start(f32[4,1024]{1,0:T(4,128)} %param.17) | copy-start | bytes 49156
Sparse Core Ops, SparseCore 0:
  35.1 148.7 all-reduce.1
where the time goes:
time: 226 us
  waiting for transfers between devices  157 us (69%)
  matrix products  22.6 us (10%)
  other arithmetic  17.8 us (8%)
  between operations  14.2 us (6%)
  starting transfers between devices  10.9 us (5%)
  local copies, waits for them, and re-layouts  3.84 us (2%)
    psum x1, waiting for transfers between devices, per_device(): hot_grad = lax.psum(hot_term, ('node', 'chip'))  153 us
    dot_general x2, matrix products, block_grad(): return jnp.dot(weights, arrived_rows, preferred_element_type=jnp.float32)  16.2 us
    sub x2, other arithmetic, adagrad(): weight - LEARN_RATE * grad / jnp.sqrt(accum_new)[..., None]  8.39 us
    all_to_all x1, starting transfers between devices, per_device(): lax.all_to_all(out_scale.reshape(devices, capacity), ('node', 'chip'), sp...  7.33 us
    reduce_sum x2, other arithmetic, adagrad(): accum_new = accum + jnp.mean(grad * grad, axis=-1)  6.65 us
  transfers between devices with their start and end apart: 3, of which 2 were waited for; matrix products, arithmetic and copies ran while one was open for 5% of the time, Pallas kernels for 0%

commit v1 on v0

--- a/solution.py
+++ b/solution.py
@@ -85,7 +85,7 @@
     matches = jnp.sum((hot_slot[:, :, :, None] == levels).astype(jnp.float32), axis=2)
     coeffs = (matches * grad_scale.astype(jnp.float32)[:, :, None]).astype(jnp.bfloat16)
     hot_term = jnp.einsum("sth,std->thd", coeffs, pooled_grad, preferred_element_type=jnp.float32)
-    hot_grad = lax.psum(hot_term, ("node", "chip"))
+    hot_grad = lax.psum(lax.psum(hot_term, "chip"), "node")
     hot_weight_new, hot_accum_new = adagrad(hot_weight, hot_accum, hot_grad)
     return (cold_weight_new, cold_accum_new, hot_weight_new, hot_accum_new)
 

time: 226 us -> 236 us (1.044)
  waiting for transfers between devices: 157 us -> 166 us
    psum x1 -> x2, waiting for transfers between devices: 153 us -> 163 us  [per_device(): hot_grad = lax.psum(lax.psum(hot_term, 'chip'), 'node')]
  transfers between devices with their start and end apart: 3 -> 4, of which waited for: 2 -> 3; matrix products, arithmetic and copies ran while one was open for 5% -> 5% of each run, Pallas kernels for 0% -> 0%
where the time goes in v1:
time: 236 us
  waiting for transfers between devices  166 us (70%)
  matrix products  22.6 us (10%)
  other arithmetic  17.8 us (8%)
  between operations  14.2 us (6%)
  starting transfers between devices  10.9 us (5%)
  local copies, waits for them, and re-layouts  3.89 us (2%)
    psum x2, waiting for transfers between devices, per_device(): hot_grad = lax.psum(lax.psum(hot_term, 'chip'), 'node')  163 us
    dot_general x2, matrix products, block_grad(): return jnp.dot(weights, arrived_rows, preferred_element_type=jnp.float32)  16.2 us
    sub x2, other arithmetic, adagrad(): weight - LEARN_RATE * grad / jnp.sqrt(accum_new)[..., None]  8.39 us
    all_to_all x1, starting transfers between devices, per_device(): lax.all_to_all(out_scale.reshape(devices, capacity), ('node', 'chip'), sp...  7.33 us
    reduce_sum x2, other arithmetic, adagrad(): accum_new = accum + jnp.mean(grad * grad, axis=-1)  6.65 us
  transfers between devices with their start and end apart: 4, of which 3 were waited for; matrix products, arithmetic and copies ran while one was open for 5% of the time, Pallas kernels for 0%

profile of v1, /device:TPU:0, one launch (start us, length us, event | category | flops | bytes accessed | tf_op | source)
XLA Modules:
  0.0 235.9 jit_solution(4738555439074217519)
XLA Ops:
  7.2 0.0 copy-start.5
  7.2 0.0 copy-start.4
  7.2 0.8 copy.25
  8.0 0.1 reshape.71
  8.1 1.7 fusion.8
  9.8 0.6 copy.26
  10.5 7.3 %all-to-all-start = ((bf16[32,1,128]{2,1,0:T(2,128)(2,1)}), bf16[32,1,128]{2,1,0:T(2,128)(2,1)S(1)}, u32[]{:S(2)}, u32[]{:S(2)}) async-start(bf16[32,1,128]{2,1,0:T(2,128)(2,1)} %copy.26), calls=%async_computation | async-start | bytes 32768 | tf_op jit(solution)/shard_map/all_to_all | solution.py:52
  17.8 0.9 reshape.68
  18.7 0.0 copy-start.1
  18.8 2.8 %convolution_convert_fusion = bf16[4096,256]{1,0:T(8,128)(2,1)} fusion(bf16[256,256]{1,0:T(8,128)(2,1)S(1)} %reshape.68, s32[4096]{0:T(1024)} %bitcast.35), kind=kOutput, calls=%fused_computation.10 | convolution fusion | flops 538968064 | bytes 2244608 | tf_op jit(solution)/shard_map/dot_general | solution.py:36
  21.5 0.0 copy-done.4
  21.5 0.2 convert_reduce_fusion
  21.7 0.0 copy-done.5
  21.7 3.2 %all-to-all-done = bf16[32,1,128]{2,1,0:T(2,128)(2,1)S(1)} async-done(((bf16[32,1,128]{2,1,0:T(2,128)(2,1)}), bf16[32,1,128]{2,1,0:T(2,128)(2,1)S(1)}, u32[]{:S(2)}, u32[]{:S(2)}) %all-to-all-start) | async-done | bytes 8224 | tf_op jit(solution)/shard_map/all_to_all | solution.py:52
  24.9 3.5 %all-to-all-start.1 = ((bf16[32,128,256]{2,1,0:T(8,128)(2,1)}), bf16[32,128,256]{2,1,0:T(8,128)(2,1)}, u32[]{:S(2)}, u32[]{:S(2)}) async-start(bf16[32,128,256]{2,1,0:T(8,128)(2,1)} %bitcast.7), calls=%async_computation.1 | async-start | bytes 4194304 | tf_op jit(solution)/shard_map/all_to_all | solution.py:45
  28.4 0.0 copy-start.3
  28.4 0.0 copy-start
  28.4 0.0 all-reduce.3.cloned.1.call-start
  28.5 0.0 copy-done.1
  28.5 1.9 fusion.11
  30.4 0.0 all-reduce.3.cloned.1.call-update
  30.4 0.0 all-reduce.5.cloned.1.call-start
  30.5 75.7 %all-reduce.3.cloned.1.call-done = f32[4,512,256]{2,1,0:T(8,128)} async-done(((f32[4,512,256]{2,1,0:T(8,128)}), f32[4,512,256]{2,1,0:T(8,128)}) %all-reduce.3.cloned.1.call-update) | async-done | bytes 2097168 | tf_op jit(solution)/shard_map/psum | solution.py:88
  106.2 0.0 all-reduce.5.cloned.1.call-update
  106.3 0.0 copy-start.6
  106.3 87.5 %all-reduce.5.cloned.1.call-done = f32[4,512,256]{2,1,0:T(8,128)} async-done(((f32[4,512,256]{2,1,0:T(8,128)}), f32[4,512,256]{2,1,0:T(8,128)}) %all-reduce.5.cloned.1.call-update) | async-done | bytes 2097168 | tf_op jit(solution)/shard_map/psum | solution.py:88
  193.8 1.9 multiply_reduce_fusion.1
  195.8 0.0 copy-done.3
  195.8 0.6 fusion.14
  196.4 0.0 copy-done
  196.4 3.3 %divide_subtract_fusion.1 = f32[4,512,256]{2,1,0:T(8,128)} fusion(f32[4,512,256]{2,1,0:T(8,128)S(1)} %copy-done, f32[4,512,256]{2,1,0:T(8,128)} %all-reduce.5.cloned.1.call-done, f32[4,512]{1,0:T(4,128)S(1)} %get-tuple-element.49), kind=kLoop, calls=%fused_computation.15 | loop fusion | flops 1572864 | bytes 6299648 | tf_op jit(solution)/shard_map/sub | solution.py:12
  199.6 0.0 all-to-all-done.1
  199.6 0.0 copy-done.6
  199.6 18.9 %while.10 = (s32[]{:T(128)}, f32[2,2048,256]{2,1,0:T(8,128)}, s32[2]{0:T(128)S(1)}, s32[1,32,128]{2,1,0:T(8,128)S(1)}, bf16[32,128]{1,0:T(8,128)(2,1)S(1)}, /*index=5*/bf16[4096,256]{1,0:T(8,128)(2,1)}, s32[]{:T(128)}) while((s32[]{:T(128)}, f32[2,2048,256]{2,1,0:T(8,128)}, s32[2]{0:T(128)S(1)}, s32[1,32,128]{2,1,0:T(8,128)S(1)}, ...), condition=%wide.region_1.2_spmd, body=%wide.region_0.1_spmd.sunk | while | flops 4311746560 | bytes 4235869 | solution.py:77
  199.6 0.6 dynamic_slice.5
  200.3 0.7 iota_add_fusion.2
  201.0 8.1 %fusion.22 = f32[2,2048,256]{2,1,0:T(8,128)} fusion(f32[2,2048,256]{2,1,0:T(8,128)} %get-tuple-element.100, s32[]{:T(128)} %get-tuple-element.99, bf16[4096,256]{1,0:T(8,128)(2,1)} %get-tuple-element.111, s32[4096]{0:T(1024)S(1)} %bitcast.36, s32[2048]{0:T(1024)S(1)} %iota_add_fusion.2, bf16[4096]{0:T(1024)(128)(2,1)S(1)} %bitcast.33), kind=kOutput, calls=%fused_computation.7.clone.1 | convolution fusion | flops 4311744512 | bytes 4227584 | tf_op jit(solution)/shard_map/while/body/eval_jaxpr/dot_general | solution.py:74
  209.1 0.6 dynamic_slice.5
  209.7 0.7 iota_add_fusion.2
  210.4 8.1 %fusion.22 = f32[2,2048,256]{2,1,0:T(8,128)} fusion(f32[2,2048,256]{2,1,0:T(8,128)} %get-tuple-element.100, s32[]{:T(128)} %get-tuple-element.99, bf16[4096,256]{1,0:T(8,128)(2,1)} %get-tuple-element.111, s32[4096]{0:T(1024)S(1)} %bitcast.36, s32[2048]{0:T(1024)S(1)} %iota_add_fusion.2, bf16[4096]{0:T(1024)(128)(2,1)S(1)} %bitcast.33), kind=kOutput, calls=%fused_computation.7.clone.1 | convolution fusion | flops 4311744512 | bytes 4227584 | tf_op jit(solution)/shard_map/while/body/eval_jaxpr/dot_general | solution.py:74
  218.5 0.0 copy-start.2
  218.5 4.7 %multiply_reduce_fusion = (f32[2,2048]{1,0:T(2,128)S(1)}, f32[2,2048,256]{2,1,0:T(8,128)}) fusion(f32[2,2048,256]{2,1,0:T(8,128)} %get-tuple-element.36), kind=kLoop, calls=%fused_computation.12 | loop fusion | flops 3141632 | bytes 8404992 | tf_op jit(solution)/shard_map/reduce_sum | solution.py:11
  223.3 0.0 copy-done.2
  223.3 0.6 fusion.15
  223.9 5.1 %divide_subtract_fusion = f32[4,1024,256]{2,1,0:T(8,128)} fusion(f32[4,1024,256]{2,1,0:T(8,128)} %param.16, f32[4,1024,256]{2,1,0:T(8,128)} %bitcast.30, f32[4,1024]{1,0:T(4,128)S(1)} %get-tuple-element.51), kind=kLoop, calls=%fused_computation.11 | loop fusion | flops 2097152 | bytes 12599296 | tf_op jit(solution)/shard_map/sub | solution.py:12
  (7 shorter events, 0.1 us)
Async XLA Ops:
  7.2 14.5 %copy-start.5 = (bf16[64,4]{0,1:T(4,128)(2,1)S(1)}, bf16[64,4]{0,1:T(4,128)(2,1)}, u32[]{:S(2)}) copy-start(bf16[64,4]{0,1:T(4,128)(2,1)} %param.12) | copy-start | bytes 1540
  7.2 14.3 %copy-start.4 = (s32[64,4,2]{0,2,1:T(2,128)S(1)}, s32[64,4,2]{0,2,1:T(2,128)}, u32[]{:S(2)}) copy-start(s32[64,4,2]{0,2,1:T(2,128)} %param.13) | copy-start | bytes 6148
  10.5 14.4 %all-to-all-start = ((bf16[32,1,128]{2,1,0:T(2,128)(2,1)}), bf16[32,1,128]{2,1,0:T(2,128)(2,1)S(1)}, u32[]{:S(2)}, u32[]{:S(2)}) async-start(bf16[32,1,128]{2,1,0:T(2,128)(2,1)} %copy.26), calls=%async_computation | async-start | bytes 32768 | tf_op jit(solution)/shard_map/all_to_all | solution.py:52
  18.7 9.7 %copy-start.1 = (bf16[64,4,256]{2,1,0:T(4,128)(2,1)S(1)}, bf16[64,4,256]{2,1,0:T(4,128)(2,1)}, u32[]{:S(2)}) copy-start(bf16[64,4,256]{2,1,0:T(4,128)(2,1)} %param.11) | copy-start | bytes 393220
  24.9 174.7 %all-to-all-start.1 = ((bf16[32,128,256]{2,1,0:T(8,128)(2,1)}), bf16[32,128,256]{2,1,0:T(8,128)(2,1)}, u32[]{:S(2)}, u32[]{:S(2)}) async-start(bf16[32,128,256]{2,1,0:T(8,128)(2,1)} %bitcast.7), calls=%async_computation.1 | async-start | bytes 4194304 | tf_op jit(solution)/shard_map/all_to_all | solution.py:45
  28.4 167.4 %copy-start.3 = (f32[4,512]{1,0:T(4,128)S(1)}, f32[4,512]{1,0:T(4,128)}, u32[]{:S(2)}) copy-start(f32[4,512]{1,0:T(4,128)} %param.19) | copy-start | bytes 24580
  28.4 168.0 %copy-start = (f32[4,512,256]{2,1,0:T(8,128)S(1)}, f32[4,512,256]{2,1,0:T(8,128)}, u32[]{:S(2)}) copy-start(f32[4,512,256]{2,1,0:T(8,128)} %param.18) | copy-start | bytes 6291460
  28.4 77.8 %all-reduce.3.cloned.1.call-start = ((), (), s32[]{:S(2)}) async-start(), calls=%async_computation.2 | async-start | bytes 4194304 | tf_op jit(solution)/shard_map/psum | solution.py:88
  30.4 163.4 %all-reduce.5.cloned.1.call-start = ((), (), s32[]{:S(2)}) async-start(), calls=%async_computation.3 | async-start | bytes 4194304 | tf_op jit(solution)/shard_map/psum | solution.py:88
  106.3 93.4 %copy-start.6 = (s32[1,32,128]{2,1,0:T(8,128)S(1)}, s32[1,32,128]{2,1,0:T(8,128)}, u32[]{:S(2)}) copy-start(s32[1,32,128]{2,1,0:T(8,128)} %param.15) | copy-start | bytes 49156
  218.5 4.8 %copy-start.2 = (f32[4,1024]{1,0:T(4,128)S(1)}, f32[4,1024]{1,0:T(4,128)}, u32[]{:S(2)}) copy-start(f32[4,1024]{1,0:T(4,128)} %param.17) | copy-start | bytes 49156
Sparse Core Ops, SparseCore 0:
  33.0 73.1 all-reduce.2
  108.6 85.1 all-reduce.4
